TPU v7x, 32 devices: a whole 2x2x4 slice. The times are simulated.
32 devices in a mesh: groups: 2 (over y), context: 16 (over z, x, core).
Axes of the slice: x: 2, y: 2, z: 4, core: 2. Of those that a mesh axis runs over, the one named last changes fastest.
Arguments:
- query_proj: bfloat16 [4096, 5120], P(('groups', 'context')), parts along dimension 0, may hold values from -100 to 100
- key_proj: bfloat16 [4096, 1024], P(('groups', 'context')), parts along dimension 0, may hold values from -100 to 100
- values: bfloat16 [4096, 1024], P(('groups', 'context')), parts along dimension 0, may hold values from -6 to 6
- grad_out: bfloat16 [4096, 5120], P(('groups', 'context')), parts along dimension 0, may hold values from -6 to 6
- query_gain: float32 [5120], replicated, may hold values from 0.1 to 1.9
- key_gain: float32 [1024], replicated, may hold values from 0.1 to 1.9
- segments: int32 [4096], P('groups'), parts along dimension 0, may hold values from 0 to 7, never falling along the last dimension, each value on 1 to 512 neighbouring positions
- layout: int32 [64], P('groups'), parts along dimension 0, may hold values from 0 to 31, as said below
Outputs:
- query_grad: bfloat16 [4096, 5120], P(('groups', 'context')), parts along dimension 0
- key_grad: bfloat16 [4096, 1024], P(('groups', 'context')), parts along dimension 0
- value_grad: bfloat16 [4096, 1024], P(('groups', 'context')), parts along dimension 0
- query_gain_grad: float32 [10240], P('groups'), parts along dimension 0
- key_gain_grad: float32 [2048], P('groups'), parts along dimension 0
There are 2 independent parts, one for each index of `groups`. A program takes and returns all parts, laid end to end along the dimension named above; an argument that names none is the same for every part. Nothing has to cross between parts.
Inputs may be any that keep to these rules, and one draw needn't show every extreme that they name: layout is a permutation of the spans; slots are ordered device by device, 2 to a device, and each aligned run of 8 slots holds the spans of one sequence of 512 positions in some order. `segments`: document numbers never fall along the stream; a document has 1 to 512 positions, and one has exactly 512.
All inputs are finite; a program needn't handle non-finite values.
Results may differ from a plain program's by a relative error of at most 0.0086.
Values may be sent and summed in bfloat16 or wider, within the bound.
A program may use at most 128 MiB of HBM per device.

v0:
```python
import functools
import math
import jax
import jax.numpy as jnp
import numpy as np
from jax import lax
from jax.experimental import pallas as pl
from jax.experimental.pallas import tpu as pltpu
from jax.sharding import PartitionSpec as P

HD = 128
KVH = 8
SPAN = 64
SEQ = 4
LENGTH = 512
EPS = 1e-06
AHEAD = 1
BASE = 500000.0
F32 = jnp.float32
BF16 = jnp.bfloat16


def rope_tables():
    half = HD // 2
    freq = BASE ** (-2.0 * np.arange(half, dtype=np.float64) / HD)
    freq = np.concatenate([freq, freq])
    sign = np.concatenate([-np.ones(half), np.ones(half)])
    off = np.arange(SPAN)[:, None] * freq[None, :]
    start = np.arange(LENGTH // SPAN)[:, None] * SPAN * freq[None, :]
    return (
        np.stack([np.cos(off), np.sin(off) * sign]).astype(np.float32),
        np.stack([np.cos(start), np.sin(start) * sign]).astype(np.float32),
    )


def kernel(
    n_seq,
    layout_h, seg_h, q_h, k_h, v_h, g_h, qgain_h, kgain_h, t_off_h, t_start_h,
    qg_out, kg_out, vg_out, qgg_out, kgg_out,
    kv, bias, cs, qs, gs, u, r0, r2, rs13, rr13, rs2, rr2, gseq, gz,
    s_x, r_x, s_c, r_c, s_f, r_f, s_13, r_13, s_2, r_2, s_g, r_g, s_z, r_z,
    layout, seg, q_in, k_in, g_in, qgain, kgain, t_off, t_start, l_sem, v_sem,
):
    rows = q_in.shape[0]
    qw = q_in.shape[1]
    kw = k_in.shape[1]
    group = qw // kw
    spans = rows // SPAN
    per_seq = LENGTH // SPAN
    gw = group * HD
    nq = qw // HD
    scale = HD ** (-0.5)
    me = lax.axis_index("context")
    rank = lax.rem(me, SEQ)
    base = me - rank
    my_seq = base // SEQ

    def flip(bit):
        if bit == 1:
            return rank + 1 - 2 * lax.rem(rank, 2)
        if bit == 2:
            return lax.rem(rank + 2, 4)
        return 3 - rank

    peer = {j: base + flip(j) for j in (1, 2, 3)}
    zpeer = [lax.rem(my_seq + i, n_seq) for i in range(1, n_seq)]

    def rcopy(src, dst, ss, rs, dev):
        return pltpu.make_async_remote_copy(
            src_ref=src, dst_ref=dst, send_sem=ss, recv_sem=rs,
            device_id={"context": dev}, device_id_type=pl.DeviceIdType.MESH,
        )

    barrier = pltpu.get_barrier_semaphore()
    for j in (1, 2, 3):
        pl.semaphore_signal(barrier, inc=1, device_id={"context": peer[j]}, device_id_type=pl.DeviceIdType.MESH)
    for z in zpeer:
        pl.semaphore_signal(barrier, inc=1, device_id={"context": z * SEQ + rank}, device_id_type=pl.DeviceIdType.MESH)

    pairs = [
        (k_h, k_in), (layout_h, layout), (t_start_h, t_start), (t_off_h, t_off), (kgain_h, kgain),
        (seg_h, seg), (qgain_h, qgain), (q_h, q_in), (g_h, g_in),
    ]
    loads = [pltpu.make_async_copy(a, b, l_sem.at[i]) for i, (a, b) in enumerate(pairs)]
    v_loads = [
        pltpu.make_async_copy(v_h.at[:, pl.ds(h * HD, HD)], kv.at[h, 0, 1], v_sem.at[h]) for h in range(KVH)
    ]
    for c in loads[:5] + v_loads + loads[5:]:
        c.start()

    owners = [me, peer[1], peer[2], peer[3]]

    def factors(j):
        for i in range(spans):
            span = lax.rem(layout[owners[j] * spans + i], per_seq)
            c1, s1 = t_start[0, pl.ds(span, 1), :], t_start[1, pl.ds(span, 1), :]
            c2, s2 = t_off[0], t_off[1]
            cs[j, 0, i * SPAN : (i + 1) * SPAN, :] = c1 * c2 - s1 * s2
            cs[j, 1, i * SPAN : (i + 1) * SPAN, :] = s1 * c2 + c1 * s2

    def rot(x):
        return x * cs[0, 0] + pltpu.roll(x, HD // 2, 1) * cs[0, 1]

    def unrot(x, j=0):
        return x * cs[j, 0] - pltpu.roll(x, HD // 2, 1) * cs[j, 1]

    for c in loads[:5]:
        c.wait()
    factors(0)
    kf = k_in[...].astype(F32)
    rk = lax.rsqrt(jnp.sum(kf * kf, axis=1, keepdims=True) / kw + EPS)
    def x_copy(h, t):
        return rcopy(kv.at[h, 0, t], kv.at[h, 2, t], s_x.at[h, t], r_x.at[h, t], peer[2])

    def c_copy(h):
        return rcopy(kv.at[h, 0], kv.at[h, 1], s_c.at[h], r_c.at[h], peer[1])

    def f_copy(h):
        return rcopy(kv.at[h, 2], kv.at[h, 3], s_f.at[h], r_f.at[h], peer[1])

    def copy13(h):
        return rcopy(rs13.at[h], rr13.at[h], s_13.at[h], r_13.at[h], peer[1])

    def copy2(h):
        return rcopy(rs2.at[h], rr2.at[h], s_2.at[h], r_2.at[h], peer[2])

    def send_v(h):
        v_loads[h].wait()
        x_copy(h, 1).start()

    pl.semaphore_wait(barrier, 3 + n_seq - 1)
    for h in range(AHEAD):
        send_v(h)
    for h in range(KVH):
        x = k_in[:, h * HD : (h + 1) * HD].astype(F32) * rk * kgain[h : h + 1, :]
        kv[h, 0, 0] = rot(x).astype(BF16)
        if h >= AHEAD:
            send_v(h)
        x_copy(h, 0).start()
        c_copy(h).start()
    for c in loads[5:]:
        c.wait()
    for j in (1, 2, 3):
        factors(j)

    lane = lax.broadcasted_iota(jnp.int32, (1, HD), 1)
    sub = lax.broadcasted_iota(jnp.int32, (rows, 1), 0)

    def docs_of(owner):
        row = jnp.zeros((1, HD), jnp.int32)
        for i in range(spans):
            sp = layout[owner * spans + i]
            src = seg[pl.ds(sp // 2, 1), :]
            swp = pltpu.roll(src, SPAN, 1)
            want = jnp.where(lax.rem(sp, 2) == i, src, swp)
            row = jnp.where(lane // SPAN == i, want, row)
        return row

    def pos_of(owner, idx):
        out = idx
        for i in range(spans):
            out = jnp.where(idx // SPAN == i, layout[owner * spans + i] * SPAN + idx - i * SPAN, out)
        return out

    doc_q = docs_of(me)
    pos_q = pos_of(me, lane)
    doc_rows = jnp.concatenate(
        [docs_of(o).astype(F32) for o in owners] + [jnp.zeros((4, HD), F32)], axis=0
    )
    doc_cols = jnp.transpose(doc_rows)
    doc_qf = doc_q.astype(F32)
    for j in range(SEQ):
        ok = (doc_cols[:, j : j + 1] == doc_qf) & (pos_of(owners[j], sub) <= pos_q)
        bias[j * rows : (j + 1) * rows, :] = jnp.where(ok, 0.0, -jnp.inf).astype(F32)

    ssq = jnp.zeros((rows, HD), F32)
    for i in range(nq):
        x = q_in[:, i * HD : (i + 1) * HD].astype(F32)
        ssq = ssq + x * x
    rq = lax.rsqrt(jnp.sum(ssq, axis=1, keepdims=True) / qw + EPS)

    x_copy(0, 0).wait_recv()
    x_copy(0, 1).wait_recv()
    f_copy(0).start()

    def relay(h):
        copy13(h).wait_recv()
        rs2[h] = (r2[h] + rr13[h, 1].astype(F32)).astype(BF16)
        r0[h] = r0[h] + rr13[h, 0].astype(F32)
        copy2(h).start()

    def head(h, acc):
        @pl.when(h + 1 < KVH)
        def _():
            x_copy(h + 1, 0).wait_recv()
            x_copy(h + 1, 1).wait_recv()
            f_copy(h + 1).start()

        for g in range(group):
            at = pl.multiple_of(h * gw + g * HD, HD)
            x = q_in[:, pl.ds(at, HD)].astype(F32) * rq * qgain[pl.ds(h * group + g, 1), :]
            qs[g * rows : (g + 1) * rows, :] = rot(x).astype(BF16)
            gs[g * rows : (g + 1) * rows, :] = g_in[:, pl.ds(at, HD)]
        c_copy(h).wait_recv()
        f_copy(h).wait_recv()
        keys = kv[h, :, 0].reshape(SEQ * rows, HD)
        vals = kv[h, :, 1].reshape(SEQ * rows, HD)
        qv, gv = qs[...], gs[...]
        nt = (((1,), (1,)), ((), ()))
        tn = (((0,), (0,)), ((), ()))
        s = lax.dot_general(keys, qv, nt, preferred_element_type=F32)
        b = bias[...]
        s = s * (scale * math.log2(math.e)) + jnp.concatenate([b] * group, axis=1)
        e = jnp.exp2(s - jnp.max(s, axis=0, keepdims=True))
        p = e * (1.0 / jnp.sum(e, axis=0, keepdims=True))
        dp = lax.dot_general(vals, gv, nt, preferred_element_type=F32)
        delta = jnp.sum(p * dp, axis=0, keepdims=True)
        ds16 = (p * (dp - delta)).astype(BF16)
        p16 = p.astype(BF16)
        dk = jnp.dot(ds16, qv, preferred_element_type=F32) * scale
        dv = jnp.dot(p16, gv, preferred_element_type=F32)
        r0[h, 0] = dk[:rows]
        r0[h, 1] = dv[:rows]
        rs13[h, 0, 0] = dk[rows : 2 * rows].astype(BF16)
        rs13[h, 0, 1] = dv[rows : 2 * rows].astype(BF16)
        r2[h, 0] = dk[2 * rows : 3 * rows]
        r2[h, 1] = dv[2 * rows : 3 * rows]
        rs13[h, 1, 0] = dk[3 * rows :].astype(BF16)
        rs13[h, 1, 1] = dv[3 * rows :].astype(BF16)
        copy13(h).start()
        kpart = jnp.zeros((rows, HD), F32)
        for j in range(SEQ):
            kpart = kpart + unrot(dk[j * rows : (j + 1) * rows], j) * unrot(kv[h, j, 0].astype(F32), j)
        gz[my_seq, pl.ds(nq + h, 1), :] = jnp.sum(kpart, axis=0, keepdims=True) / kgain[pl.ds(h, 1), :]
        dq_t = lax.dot_general(keys, ds16, tn, preferred_element_type=F32) * scale
        for g in range(group):
            at = pl.multiple_of(h * gw + g * HD, HD)
            dqn = unrot(jnp.transpose(dq_t[:, g * HD : (g + 1) * HD]))
            x = q_in[:, pl.ds(at, HD)].astype(F32)
            w = dqn * qgain[pl.ds(h * group + g, 1), :]
            u[:, pl.ds(at, HD)] = w
            acc = acc + w * x
            gz[my_seq, pl.ds(h * group + g, 1), :] = jnp.sum(dqn * x * rq, axis=0, keepdims=True)

        @pl.when(h > 0)
        def _():
            relay(h - 1)

        return acc

    acc = lax.fori_loop(0, KVH, head, jnp.zeros((rows, HD), F32))
    def gc_copy():
        return rcopy(gseq.at[0], gseq.at[1], s_g.at[0], r_g.at[0], peer[1])

    def gx_copy():
        return rcopy(gseq.at[2], gseq.at[3], s_g.at[1], r_g.at[1], peer[2])

    def z_copy(i):
        return rcopy(gz.at[my_seq], gz.at[my_seq], s_z.at[i], r_z.at[i], zpeer[i] * SEQ + rank)

    def z_recv(i):
        src = lax.rem(my_seq + n_seq - 1 - i, n_seq)
        return rcopy(gz.at[my_seq], gz.at[src], s_z.at[i], r_z.at[i], src * SEQ + rank)

    for i in range(n_seq - 1):
        z_copy(i).start()
    relay(KVH - 1)
    inner = jnp.sum(acc, axis=1, keepdims=True) / qw * rq * rq * rq
    for i in range(nq):
        sl = slice(i * HD, (i + 1) * HD)
        qg_out[:, sl] = (rq * u[:, sl] - q_in[:, sl].astype(F32) * inner).astype(BF16)

    for i in range(n_seq - 1):
        z_recv(i).wait_recv()
    total = gz[0]
    for s_i in range(1, n_seq):
        total = total + gz[s_i]
    gseq[0] = total
    gc_copy().start()
    gc_copy().wait_recv()
    gseq[2] = gseq[0] + gseq[1]
    gx_copy().start()

    kacc = jnp.zeros((rows, HD), F32)
    for h in range(KVH):
        sl = slice(h * HD, (h + 1) * HD)
        copy2(h).wait_recv()
        vg_out[:, sl] = (r0[h, 1] + rr2[h, 1].astype(F32)).astype(BF16)
        dkn = unrot(r0[h, 0] + rr2[h, 0].astype(F32))
        x = k_in[:, sl].astype(F32)
        w = dkn * kgain[h : h + 1, :]
        r2[h, 0] = w
        kacc = kacc + w * x

    kinner = jnp.sum(kacc, axis=1, keepdims=True) / kw * rk * rk * rk
    for h in range(KVH):
        sl = slice(h * HD, (h + 1) * HD)
        kg_out[:, sl] = (rk * r2[h, 0] - k_in[:, sl].astype(F32) * kinner).astype(BF16)

    gx_copy().wait_recv()
    total = gseq[2] + gseq[3]
    qgg_out[...] = total[:nq]
    kgg_out[...] = total[nq:]

    for h in range(KVH):
        x_copy(h, 0).wait_send()
        x_copy(h, 1).wait_send()
        c_copy(h).wait_send()
        f_copy(h).wait_send()
        copy13(h).wait_send()
        copy2(h).wait_send()
    gc_copy().wait_send()
    gx_copy().wait_send()
    for i in range(n_seq - 1):
        z_copy(i).wait_send()


def flush(*refs):
    sems = refs[10]
    copies = [pltpu.make_async_copy(refs[i], refs[5 + i], sems.at[i]) for i in range(5)]
    for c in copies:
        c.start()
    for c in copies:
        c.wait()


def body(n_ctx, query_proj, key_proj, values, grad_out, query_gain, key_gain, segments, layout):
    rows, qw = query_proj.shape
    kw = key_proj.shape[1]
    group = qw // kw
    n_seq = n_ctx // SEQ
    nq, nk = qw // HD, kw // HD
    t_off, t_start = rope_tables()
    vmem = pl.BlockSpec(memory_space=pltpu.VMEM)
    sem = pltpu.SemaphoreType.DMA
    outs = pl.pallas_call(
        functools.partial(kernel, n_seq),
        out_shape=(
            pltpu.VMEM((rows, qw), BF16),
            pltpu.VMEM((rows, kw), BF16),
            pltpu.VMEM((rows, kw), BF16),
            pltpu.VMEM((nq, HD), F32),
            pltpu.VMEM((nk, HD), F32),
        ),
        in_specs=[pl.BlockSpec(memory_space=pltpu.HBM)] * 10,
        out_specs=(vmem,) * 5,
        scratch_shapes=[
            pltpu.VMEM((nk, SEQ, 2, rows, HD), BF16),
            pltpu.VMEM((SEQ * rows, rows), F32),
            pltpu.VMEM((SEQ, 2, rows, HD), F32),
            pltpu.VMEM((group * rows, HD), BF16),
            pltpu.VMEM((group * rows, HD), BF16),
            pltpu.VMEM((rows, qw), F32),
            pltpu.VMEM((nk, 2, rows, HD), F32),
            pltpu.VMEM((nk, 2, rows, HD), F32),
            pltpu.VMEM((nk, 2, 2, rows, HD), BF16),
            pltpu.VMEM((nk, 2, 2, rows, HD), BF16),
            pltpu.VMEM((nk, 2, rows, HD), BF16),
            pltpu.VMEM((nk, 2, rows, HD), BF16),
            pltpu.VMEM((SEQ, nq + nk, HD), F32),
            pltpu.VMEM((n_seq, nq + nk, HD), F32),
        ]
        + [sem((nk, 2))] * 2
        + [sem((nk,))] * 8
        + [sem((2,))] * 2
        + [sem((max(n_seq - 1, 1),))] * 2
        + [
            pltpu.SMEM(layout.shape, jnp.int32),
            pltpu.VMEM((segments.shape[0] // HD, HD), jnp.int32),
            pltpu.VMEM((rows, qw), BF16),
            pltpu.VMEM((rows, kw), BF16),
            pltpu.VMEM((rows, qw), BF16),
            pltpu.VMEM((nq, HD), F32),
            pltpu.VMEM((nk, HD), F32),
            pltpu.VMEM(t_off.shape, F32),
            pltpu.VMEM(t_start.shape, F32),
            sem((9,)),
            sem((nk,)),
        ],
        compiler_params=pltpu.CompilerParams(
            collective_id=0, has_side_effects=True, vmem_limit_bytes=65100000
        ),
    )(
        layout, segments.reshape(-1, HD), query_proj, key_proj, values, grad_out,
        query_gain.reshape(nq, HD), key_gain.reshape(nk, HD), jnp.asarray(t_off), jnp.asarray(t_start),
    )
    anyspace = pl.BlockSpec(memory_space=pl.ANY)
    outs = pl.pallas_call(
        flush,
        out_shape=tuple(jax.ShapeDtypeStruct(o.shape, o.dtype) for o in outs),
        in_specs=[anyspace] * 5,
        out_specs=(anyspace,) * 5,
        scratch_shapes=[sem((5,))],
        compiler_params=pltpu.CompilerParams(vmem_limit_bytes=8 * 1024 * 1024),
    )(*outs)
    return outs[0], outs[1], outs[2], outs[3].reshape(qw), outs[4].reshape(kw)


def solution(mesh):
    tok = P(("groups", "context"), None)
    return jax.shard_map(
        functools.partial(body, mesh.shape["context"]),
        mesh=mesh,
        in_specs=(tok, tok, tok, tok, P(), P(), P("groups"), P("groups")),
        out_specs=(tok, tok, tok, P("groups"), P("groups")),
        check_vma=False,
    )
```

profile of v0, /device:TPU:0, one launch (start us, length us, event | category | flops | bytes accessed | tf_op | source)
XLA Modules:
  0.0 34.7 jit_solution(6197814324238433111)
XLA Ops:
  0.6 32.8 %shard_map.137 = (bf16[128,5120]{1,0:T(8,128)(2,1)S(1)}, bf16[128,1024]{1,0:T(8,128)(2,1)S(1)}, bf16[128,1024]{1,0:T(8,128)(2,1)S(1)}, f32[40,128]{1,0:T(8,128)S(1)}, f32[8,128]{1,0:T(8,128)S(1)}) custom-call(s32[32]{0:T(128)} %layout_h.1, s32[16,128]{1,0:T(8,128)} %bitcast.6, bf16[128,5120]{1,0:T(8,128)(2,1)} %q_h.1, bf16[128,1024]{1,0:T(8,128)(2,1)} %k_h.1, ...), custom_call_target="tpu_custom_call" | custom-call | tf_op jit(solution)/shard_map/pallas_call | solution.py:336
  33.4 1.3 %shard_map.138 = (bf16[128,5120]{1,0:T(8,128)(2,1)}, bf16[128,1024]{1,0:T(8,128)(2,1)}, bf16[128,1024]{1,0:T(8,128)(2,1)}, f32[40,128]{1,0:T(8,128)}, f32[8,128]{1,0:T(8,128)}) custom-call(bf16[128,5120]{1,0:T(8,128)(2,1)S(1)} %get-tuple-element.15.refs_0_, bf16[128,1024]{1,0:T(8,128)(2,1)S(1)} %get-tuple-element.16.refs_1_, ...), custom_call_target="tpu_custom_call" | custom-call | tf_op jit(solution)/shard_map/pallas_call | solution.py:388
where the time goes:
time: 34.9 us; the launch traced here: 34.7 us
  Pallas kernels  34.1 us (98%)
  between operations  0.64 us (2%)
    pallas_call x1, Pallas kernels, body(): pl.pallas_call(functools.partial(kernel, n_seq), out_shape=(pltpu.VMEM((r...  32.8 us
    pallas_call x1, Pallas kernels, body(): pl.pallas_call(flush, out_shape=tuple((jax.ShapeDtypeStruct(o.shape, o.dt...  1.27 us

commit v1 on v0

--- a/solution.py
+++ b/solution.py
@@ -14,7 +14,8 @@
 SEQ = 4
 LENGTH = 512
 EPS = 1e-06
-AHEAD = 1
+AHEAD = 2
+CHUNK = 2
 BASE = 500000.0
 F32 = jnp.float32
 BF16 = jnp.bfloat16
@@ -37,9 +38,9 @@
     n_seq,
     layout_h, seg_h, q_h, k_h, v_h, g_h, qgain_h, kgain_h, t_off_h, t_start_h,
     qg_out, kg_out, vg_out, qgg_out, kgg_out,
-    kv, bias, cs, qs, gs, u, r0, r2, rs13, rr13, rs2, rr2, gseq, gz,
+    kv, bias, cs, qs, gs, u, r0, r2, rs13, rr13, rs2, rr2, gseq, gz, ds_a, p_a, ds_b, p_b, accq, rqb,
     s_x, r_x, s_c, r_c, s_f, r_f, s_13, r_13, s_2, r_2, s_g, r_g, s_z, r_z,
-    layout, seg, q_in, k_in, g_in, qgain, kgain, t_off, t_start, l_sem, v_sem,
+    layout, seg, q_in, k_in, g_in, qgain, kgain, t_off, t_start, l_sem, v_sem, ready, z_ready, z_known,
 ):
     rows = q_in.shape[0]
     qw = q_in.shape[1]
@@ -54,6 +55,7 @@
     rank = lax.rem(me, SEQ)
     base = me - rank
     my_seq = base // SEQ
+    lead = lax.rem(rank, 2) == 1
 
     def flip(bit):
         if bit == 1:
@@ -63,7 +65,7 @@
         return 3 - rank
 
     peer = {j: base + flip(j) for j in (1, 2, 3)}
-    zpeer = [lax.rem(my_seq + i, n_seq) for i in range(1, n_seq)]
+    zpeer = [lax.rem(my_seq + i, n_seq) * SEQ + rank for i in range(1, n_seq)]
 
     def rcopy(src, dst, ss, rs, dev):
         return pltpu.make_async_remote_copy(
@@ -71,11 +73,21 @@
             device_id={"context": dev}, device_id_type=pl.DeviceIdType.MESH,
         )
 
+    def tell(sem, dev):
+        pl.semaphore_signal(sem, inc=1, device_id={"context": dev}, device_id_type=pl.DeviceIdType.MESH)
+
     barrier = pltpu.get_barrier_semaphore()
-    for j in (1, 2, 3):
-        pl.semaphore_signal(barrier, inc=1, device_id={"context": peer[j]}, device_id_type=pl.DeviceIdType.MESH)
-    for z in zpeer:
-        pl.semaphore_signal(barrier, inc=1, device_id={"context": z * SEQ + rank}, device_id_type=pl.DeviceIdType.MESH)
+
+    @pl.when(lead)
+    def _():
+        tell(barrier, peer[1])
+        tell(barrier, peer[3])
+        for z in zpeer:
+            tell(barrier, z)
+
+    @pl.when(jnp.logical_not(lead))
+    def _():
+        tell(barrier, peer[2])
 
     pairs = [
         (k_h, k_in), (layout_h, layout), (t_start_h, t_start), (t_off_h, t_off), (kgain_h, kgain),
@@ -109,6 +121,7 @@
     factors(0)
     kf = k_in[...].astype(F32)
     rk = lax.rsqrt(jnp.sum(kf * kf, axis=1, keepdims=True) / kw + EPS)
+
     def x_copy(h, t):
         return rcopy(kv.at[h, 0, t], kv.at[h, 2, t], s_x.at[h, t], r_x.at[h, t], peer[2])
 
@@ -124,18 +137,29 @@
     def copy2(h):
         return rcopy(rs2.at[h], rr2.at[h], s_2.at[h], r_2.at[h], peer[2])
 
-    def send_v(h):
-        v_loads[h].wait()
-        x_copy(h, 1).start()
-
-    pl.semaphore_wait(barrier, 3 + n_seq - 1)
-    for h in range(AHEAD):
-        send_v(h)
-    for h in range(KVH):
+    def prepare_k(h):
         x = k_in[:, h * HD : (h + 1) * HD].astype(F32) * rk * kgain[h : h + 1, :]
         kv[h, 0, 0] = rot(x).astype(BF16)
+
+    for h in range(AHEAD):
+        prepare_k(h)
+    for h in range(AHEAD):
+        v_loads[h].wait()
+
+    @pl.when(jnp.logical_not(lead))
+    def _():
+        pl.semaphore_wait(barrier, 3)
+        tell(ready, peer[1])
+
+    @pl.when(lead)
+    def _():
+        pl.semaphore_wait(ready, 1)
+
+    for h in range(KVH):
         if h >= AHEAD:
-            send_v(h)
+            prepare_k(h)
+            v_loads[h].wait()
+        x_copy(h, 1).start()
         x_copy(h, 0).start()
         c_copy(h).start()
     for c in loads[5:]:
@@ -178,10 +202,31 @@
         x = q_in[:, i * HD : (i + 1) * HD].astype(F32)
         ssq = ssq + x * x
     rq = lax.rsqrt(jnp.sum(ssq, axis=1, keepdims=True) / qw + EPS)
-
-    x_copy(0, 0).wait_recv()
-    x_copy(0, 1).wait_recv()
-    f_copy(0).start()
+    rqb[...] = jnp.broadcast_to(rq, (rows, HD))
+    accq[...] = jnp.zeros((rows, HD), F32)
+
+    def prepare_q(h, carry):
+        for g in range(group):
+            at = pl.multiple_of(h * gw + g * HD, HD)
+            x = q_in[:, pl.ds(at, HD)].astype(F32) * rqb[...] * qgain[pl.ds(h * group + g, 1), :]
+            qs[h, g * rows : (g + 1) * rows, :] = rot(x).astype(BF16)
+            gs[h, g * rows : (g + 1) * rows, :] = g_in[:, pl.ds(at, HD)]
+        return carry
+
+    lax.fori_loop(0, KVH, prepare_q, 0)
+
+    nt = (((1,), (1,)), ((), ()))
+    tn = (((0,), (0,)), ((), ()))
+    chunks = [(a, min(a + CHUNK, group)) for a in range(0, group, CHUNK)]
+
+    def forward(h):
+        x_copy(h, 0).wait_recv()
+        x_copy(h, 1).wait_recv()
+        f_copy(h).start()
+
+    def arrive(h):
+        c_copy(h).wait_recv()
+        f_copy(h).wait_recv()
 
     def relay(h):
         copy13(h).wait_recv()
@@ -189,50 +234,51 @@
         r0[h] = r0[h] + rr13[h, 0].astype(F32)
         copy2(h).start()
 
-    def head(h, acc):
-        @pl.when(h + 1 < KVH)
-        def _():
-            x_copy(h + 1, 0).wait_recv()
-            x_copy(h + 1, 1).wait_recv()
-            f_copy(h + 1).start()
-
-        for g in range(group):
-            at = pl.multiple_of(h * gw + g * HD, HD)
-            x = q_in[:, pl.ds(at, HD)].astype(F32) * rq * qgain[pl.ds(h * group + g, 1), :]
-            qs[g * rows : (g + 1) * rows, :] = rot(x).astype(BF16)
-            gs[g * rows : (g + 1) * rows, :] = g_in[:, pl.ds(at, HD)]
-        c_copy(h).wait_recv()
-        f_copy(h).wait_recv()
+    def scores(h, a, b):
         keys = kv[h, :, 0].reshape(SEQ * rows, HD)
         vals = kv[h, :, 1].reshape(SEQ * rows, HD)
-        qv, gv = qs[...], gs[...]
-        nt = (((1,), (1,)), ((), ()))
-        tn = (((0,), (0,)), ((), ()))
-        s = lax.dot_general(keys, qv, nt, preferred_element_type=F32)
-        b = bias[...]
-        s = s * (scale * math.log2(math.e)) + jnp.concatenate([b] * group, axis=1)
+        cols = slice(a * rows, b * rows)
+        s = lax.dot_general(keys, qs[h, cols, :], nt, preferred_element_type=F32)
+        dp = lax.dot_general(vals, gs[h, cols, :], nt, preferred_element_type=F32)
+        return s, dp
+
+    def weights(s, dp, a, b, ds_ref, p_ref):
+        cols = slice(a * rows, b * rows)
+        s = s * (scale * math.log2(math.e)) + jnp.concatenate([bias[...]] * (b - a), axis=1)
         e = jnp.exp2(s - jnp.max(s, axis=0, keepdims=True))
         p = e * (1.0 / jnp.sum(e, axis=0, keepdims=True))
-        dp = lax.dot_general(vals, gv, nt, preferred_element_type=F32)
         delta = jnp.sum(p * dp, axis=0, keepdims=True)
-        ds16 = (p * (dp - delta)).astype(BF16)
-        p16 = p.astype(BF16)
-        dk = jnp.dot(ds16, qv, preferred_element_type=F32) * scale
-        dv = jnp.dot(p16, gv, preferred_element_type=F32)
+        ds_ref[:, cols] = (p * (dp - delta)).astype(BF16)
+        p_ref[:, cols] = p.astype(BF16)
+
+    def softmax(h, ds_ref, p_ref):
+        for a, b in chunks:
+            weights(*scores(h, a, b), a, b, ds_ref, p_ref)
+
+    def key_products(h, ds_ref, p_ref):
+        dk = jnp.dot(ds_ref[...], qs[h], preferred_element_type=F32) * scale
         r0[h, 0] = dk[:rows]
-        r0[h, 1] = dv[:rows]
         rs13[h, 0, 0] = dk[rows : 2 * rows].astype(BF16)
-        rs13[h, 0, 1] = dv[rows : 2 * rows].astype(BF16)
         r2[h, 0] = dk[2 * rows : 3 * rows]
-        r2[h, 1] = dv[2 * rows : 3 * rows]
         rs13[h, 1, 0] = dk[3 * rows :].astype(BF16)
-        rs13[h, 1, 1] = dv[3 * rows :].astype(BF16)
-        copy13(h).start()
         kpart = jnp.zeros((rows, HD), F32)
         for j in range(SEQ):
             kpart = kpart + unrot(dk[j * rows : (j + 1) * rows], j) * unrot(kv[h, j, 0].astype(F32), j)
         gz[my_seq, pl.ds(nq + h, 1), :] = jnp.sum(kpart, axis=0, keepdims=True) / kgain[pl.ds(h, 1), :]
-        dq_t = lax.dot_general(keys, ds16, tn, preferred_element_type=F32) * scale
+
+    def value_products(h, p_ref):
+        dv = jnp.dot(p_ref[...], gs[h], preferred_element_type=F32)
+        r0[h, 1] = dv[:rows]
+        rs13[h, 0, 1] = dv[rows : 2 * rows].astype(BF16)
+        r2[h, 1] = dv[2 * rows : 3 * rows]
+        rs13[h, 1, 1] = dv[3 * rows :].astype(BF16)
+
+    def query_products(h, ds_ref):
+        keys = kv[h, :, 0].reshape(SEQ * rows, HD)
+        return lax.dot_general(keys, ds_ref[...], tn, preferred_element_type=F32) * scale
+
+    def query_side(h, dq_t):
+        acc = accq[...]
         for g in range(group):
             at = pl.multiple_of(h * gw + g * HD, HD)
             dqn = unrot(jnp.transpose(dq_t[:, g * HD : (g + 1) * HD]))
@@ -240,15 +286,75 @@
             w = dqn * qgain[pl.ds(h * group + g, 1), :]
             u[:, pl.ds(at, HD)] = w
             acc = acc + w * x
-            gz[my_seq, pl.ds(h * group + g, 1), :] = jnp.sum(dqn * x * rq, axis=0, keepdims=True)
-
-        @pl.when(h > 0)
+            gz[my_seq, pl.ds(h * group + g, 1), :] = jnp.sum(dqn * x * rqb[...], axis=0, keepdims=True)
+        accq[...] = acc
+
+    slots = ((ds_a, p_a), (ds_b, p_b))
+
+    def step(h, now, nxt):
+        sc = scores(h + 1, *chunks[0])
+        dq_t = query_products(h, now[0])
+        weights(*sc, *chunks[0], *nxt)
+        sc = scores(h + 1, *chunks[1])
+        key_products(h, *now)
+        query_side(h, dq_t)
+        weights(*sc, *chunks[1], *nxt)
+        sc = scores(h + 1, *chunks[2])
+        value_products(h, now[1])
+        weights(*sc, *chunks[2], *nxt)
+        copy13(h).start()
+
+    def meet(h):
+        forward(h + 1)
+        arrive(h)
+
+    forward(0)
+    arrive(0)
+    softmax(0, *slots[0])
+    forward(1)
+
+    def two(i, carry):
+        h = 2 * i
+        meet(h + 1)
+
+        @pl.when(i > 0)
         def _():
             relay(h - 1)
 
-        return acc
-
-    acc = lax.fori_loop(0, KVH, head, jnp.zeros((rows, HD), F32))
+        step(h, slots[0], slots[1])
+        meet(h + 2)
+        relay(h)
+        step(h + 1, slots[1], slots[0])
+        return carry
+
+    half = (KVH - 2) // 2
+    lax.fori_loop(0, half, two, 0)
+
+    @pl.when(lead)
+    def _():
+        pl.semaphore_wait(barrier, n_seq - 1)
+        for z in zpeer:
+            tell(z_ready, z)
+
+    arrive(KVH - 1)
+    relay(KVH - 3)
+    step(KVH - 2, slots[0], slots[1])
+
+    @pl.when(lead)
+    def _():
+        pl.semaphore_wait(z_ready, n_seq - 1)
+        tell(z_known, peer[1])
+
+    key_products(KVH - 1, *slots[1])
+    value_products(KVH - 1, slots[1][1])
+    copy13(KVH - 1).start()
+    relay(KVH - 2)
+    query_side(KVH - 1, query_products(KVH - 1, slots[1][0]))
+
+    @pl.when(jnp.logical_not(lead))
+    def _():
+        pl.semaphore_wait(z_known, 1)
+
     def gc_copy():
         return rcopy(gseq.at[0], gseq.at[1], s_g.at[0], r_g.at[0], peer[1])
 
@@ -256,7 +362,7 @@
         return rcopy(gseq.at[2], gseq.at[3], s_g.at[1], r_g.at[1], peer[2])
 
     def z_copy(i):
-        return rcopy(gz.at[my_seq], gz.at[my_seq], s_z.at[i], r_z.at[i], zpeer[i] * SEQ + rank)
+        return rcopy(gz.at[my_seq], gz.at[my_seq], s_z.at[i], r_z.at[i], zpeer[i])
 
     def z_recv(i):
         src = lax.rem(my_seq + n_seq - 1 - i, n_seq)
@@ -265,10 +371,27 @@
     for i in range(n_seq - 1):
         z_copy(i).start()
     relay(KVH - 1)
-    inner = jnp.sum(acc, axis=1, keepdims=True) / qw * rq * rq * rq
+    rq = rqb[...]
+    inner = jnp.sum(accq[...], axis=1, keepdims=True) / qw * rq * rq * rq
     for i in range(nq):
         sl = slice(i * HD, (i + 1) * HD)
         qg_out[:, sl] = (rq * u[:, sl] - q_in[:, sl].astype(F32) * inner).astype(BF16)
+
+    kacc = jnp.zeros((rows, HD), F32)
+
+    def finish(h, kacc):
+        sl = slice(h * HD, (h + 1) * HD)
+        copy2(h).wait_recv()
+        vg_out[:, sl] = (r0[h, 1] + rr2[h, 1].astype(F32)).astype(BF16)
+        dkn = unrot(r0[h, 0] + rr2[h, 0].astype(F32))
+        x = k_in[:, sl].astype(F32)
+        w = dkn * kgain[h : h + 1, :]
+        r2[h, 0] = w
+        return kacc + w * x
+
+    early = KVH - 2
+    for h in range(early):
+        kacc = finish(h, kacc)
 
     for i in range(n_seq - 1):
         z_recv(i).wait_recv()
@@ -277,20 +400,11 @@
         total = total + gz[s_i]
     gseq[0] = total
     gc_copy().start()
+    kacc = finish(early, kacc)
     gc_copy().wait_recv()
     gseq[2] = gseq[0] + gseq[1]
     gx_copy().start()
-
-    kacc = jnp.zeros((rows, HD), F32)
-    for h in range(KVH):
-        sl = slice(h * HD, (h + 1) * HD)
-        copy2(h).wait_recv()
-        vg_out[:, sl] = (r0[h, 1] + rr2[h, 1].astype(F32)).astype(BF16)
-        dkn = unrot(r0[h, 0] + rr2[h, 0].astype(F32))
-        x = k_in[:, sl].astype(F32)
-        w = dkn * kgain[h : h + 1, :]
-        r2[h, 0] = w
-        kacc = kacc + w * x
+    kacc = finish(early + 1, kacc)
 
     kinner = jnp.sum(kacc, axis=1, keepdims=True) / kw * rk * rk * rk
     for h in range(KVH):
@@ -348,8 +462,8 @@
             pltpu.VMEM((nk, SEQ, 2, rows, HD), BF16),
             pltpu.VMEM((SEQ * rows, rows), F32),
             pltpu.VMEM((SEQ, 2, rows, HD), F32),
-            pltpu.VMEM((group * rows, HD), BF16),
-            pltpu.VMEM((group * rows, HD), BF16),
+            pltpu.VMEM((nk, group * rows, HD), BF16),
+            pltpu.VMEM((nk, group * rows, HD), BF16),
             pltpu.VMEM((rows, qw), F32),
             pltpu.VMEM((nk, 2, rows, HD), F32),
             pltpu.VMEM((nk, 2, rows, HD), F32),
@@ -360,6 +474,8 @@
             pltpu.VMEM((SEQ, nq + nk, HD), F32),
             pltpu.VMEM((n_seq, nq + nk, HD), F32),
         ]
+        + [pltpu.VMEM((SEQ * rows, group * rows), BF16)] * 4
+        + [pltpu.VMEM((rows, HD), F32)] * 2
         + [sem((nk, 2))] * 2
         + [sem((nk,))] * 8
         + [sem((2,))] * 2
@@ -376,7 +492,8 @@
             pltpu.VMEM(t_start.shape, F32),
             sem((9,)),
             sem((nk,)),
-        ],
+        ]
+        + [pltpu.SemaphoreType.REGULAR] * 3,
         compiler_params=pltpu.CompilerParams(
             collective_id=0, has_side_effects=True, vmem_limit_bytes=65100000
         ),

time: 34.9 us -> 41 us (1.17)
  Pallas kernels: 34.1 us -> 40.2 us
    pallas_call x1, Pallas kernels: 32.8 us -> 38.9 us  [body(): pl.pallas_call(functools.partial(kernel, n_seq), out_shape=(pltpu.VMEM((r...]
where the time goes in v1:
time: 41 us; the launch traced here: 40.8 us
  Pallas kernels  40.2 us (98%)
  between operations  0.64 us (2%)
    pallas_call x1, Pallas kernels, body(): pl.pallas_call(functools.partial(kernel, n_seq), out_shape=(pltpu.VMEM((r...  38.9 us
    pallas_call x1, Pallas kernels, body(): pl.pallas_call(flush, out_shape=tuple((jax.ShapeDtypeStruct(o.shape, o.dt...  1.27 us

profile of v1, /device:TPU:0, one launch (start us, length us, event | category | flops | bytes accessed | tf_op | source)
XLA Modules:
  0.0 40.8 jit_solution(10626821695829328327)
XLA Ops:
  0.6 38.9 %shard_map.137 = (bf16[128,5120]{1,0:T(8,128)(2,1)S(1)}, bf16[128,1024]{1,0:T(8,128)(2,1)S(1)}, bf16[128,1024]{1,0:T(8,128)(2,1)S(1)}, f32[40,128]{1,0:T(8,128)S(1)}, f32[8,128]{1,0:T(8,128)S(1)}) custom-call(s32[32]{0:T(128)} %layout_h.1, s32[16,128]{1,0:T(8,128)} %bitcast.6, bf16[128,5120]{1,0:T(8,128)(2,1)} %q_h.1, bf16[128,1024]{1,0:T(8,128)(2,1)} %k_h.1, ...), custom_call_target="tpu_custom_call" | custom-call | tf_op jit(solution)/shard_map/pallas_call | solution.py:450
  39.6 1.3 %shard_map.138 = (bf16[128,5120]{1,0:T(8,128)(2,1)}, bf16[128,1024]{1,0:T(8,128)(2,1)}, bf16[128,1024]{1,0:T(8,128)(2,1)}, f32[40,128]{1,0:T(8,128)}, f32[8,128]{1,0:T(8,128)}) custom-call(bf16[128,5120]{1,0:T(8,128)(2,1)S(1)} %get-tuple-element.15.refs_0_, bf16[128,1024]{1,0:T(8,128)(2,1)S(1)} %get-tuple-element.16.refs_1_, ...), custom_call_target="tpu_custom_call" | custom-call | tf_op jit(solution)/shard_map/pallas_call | solution.py:505

commit v2 on v1

--- a/solution.py
+++ b/solution.py
@@ -15,7 +15,7 @@
 LENGTH = 512
 EPS = 1e-06
 AHEAD = 2
-CHUNK = 2
+CHUNK = 3
 BASE = 500000.0
 F32 = jnp.float32
 BF16 = jnp.bfloat16
@@ -38,8 +38,8 @@
     n_seq,
     layout_h, seg_h, q_h, k_h, v_h, g_h, qgain_h, kgain_h, t_off_h, t_start_h,
     qg_out, kg_out, vg_out, qgg_out, kgg_out,
-    kv, bias, cs, qs, gs, u, r0, r2, rs13, rr13, rs2, rr2, gseq, gz, ds_a, p_a, ds_b, p_b, accq, rqb,
-    s_x, r_x, s_c, r_c, s_f, r_f, s_13, r_13, s_2, r_2, s_g, r_g, s_z, r_z,
+    kv, bias, cs, qs, gs, u, r0, r2, rs13, rr13, rs2, rr2, gseq, gz, ds_a, p_a, ds_b, p_b, accq, rqb, glast,
+    s_x, s_c, s_f, s_13, s_2, s_l, r_l, r_x, r_cf, r_13, r_2, s_g, r_g, s_z, r_z,
     layout, seg, q_in, k_in, g_in, qgain, kgain, t_off, t_start, l_sem, v_sem, ready, z_ready, z_known,
 ):
     rows = q_in.shape[0]
@@ -95,12 +95,12 @@
     ]
     loads = [pltpu.make_async_copy(a, b, l_sem.at[i]) for i, (a, b) in enumerate(pairs)]
     v_loads = [
-        pltpu.make_async_copy(v_h.at[:, pl.ds(h * HD, HD)], kv.at[h, 0, 1], v_sem.at[h]) for h in range(KVH)
+        pltpu.make_async_copy(v_h.at[:, pl.ds(h * HD, HD)], kv.at[h, 0, 1], v_sem) for h in range(KVH)
     ]
     for c in loads[:5] + v_loads + loads[5:]:
         c.start()
 
-    owners = [me, peer[1], peer[2], peer[3]]
+    owners = [me, peer[2], peer[1], peer[3]]
 
     def factors(j):
         for i in range(spans):
@@ -123,19 +123,19 @@
     rk = lax.rsqrt(jnp.sum(kf * kf, axis=1, keepdims=True) / kw + EPS)
 
     def x_copy(h, t):
-        return rcopy(kv.at[h, 0, t], kv.at[h, 2, t], s_x.at[h, t], r_x.at[h, t], peer[2])
+        return rcopy(kv.at[h, 0, t], kv.at[h, 1, t], s_x, r_x.at[h], peer[2])
 
     def c_copy(h):
-        return rcopy(kv.at[h, 0], kv.at[h, 1], s_c.at[h], r_c.at[h], peer[1])
+        return rcopy(kv.at[h, 0], kv.at[h, 2], s_c, r_cf.at[h], peer[1])
 
     def f_copy(h):
-        return rcopy(kv.at[h, 2], kv.at[h, 3], s_f.at[h], r_f.at[h], peer[1])
+        return rcopy(kv.at[h, 1], kv.at[h, 3], s_f, r_cf.at[h], peer[1])
 
     def copy13(h):
-        return rcopy(rs13.at[h], rr13.at[h], s_13.at[h], r_13.at[h], peer[1])
+        return rcopy(rs13.at[h], rr13.at[h], s_13, r_13.at[h], peer[1])
 
     def copy2(h):
-        return rcopy(rs2.at[h], rr2.at[h], s_2.at[h], r_2.at[h], peer[2])
+        return rcopy(rs2.at[h], rr2.at[h], s_2, r_2.at[h], peer[2])
 
     def prepare_k(h):
         x = k_in[:, h * HD : (h + 1) * HD].astype(F32) * rk * kgain[h : h + 1, :]
@@ -143,8 +143,7 @@
 
     for h in range(AHEAD):
         prepare_k(h)
-    for h in range(AHEAD):
-        v_loads[h].wait()
+    pltpu.make_async_copy(kv.at[:, 0, 1], kv.at[:, 0, 1], v_sem).wait()
 
     @pl.when(jnp.logical_not(lead))
     def _():
@@ -158,7 +157,6 @@
     for h in range(KVH):
         if h >= AHEAD:
             prepare_k(h)
-            v_loads[h].wait()
         x_copy(h, 1).start()
         x_copy(h, 0).start()
         c_copy(h).start()
@@ -220,13 +218,11 @@
     chunks = [(a, min(a + CHUNK, group)) for a in range(0, group, CHUNK)]
 
     def forward(h):
-        x_copy(h, 0).wait_recv()
-        x_copy(h, 1).wait_recv()
+        rcopy(kv.at[h, 0], kv.at[h, 1], s_x, r_x.at[h], peer[2]).wait_recv()
         f_copy(h).start()
 
     def arrive(h):
-        c_copy(h).wait_recv()
-        f_copy(h).wait_recv()
+        rcopy(kv.at[h, pl.ds(0, 2)], kv.at[h, pl.ds(2, 2)], s_c, r_cf.at[h], peer[1]).wait_recv()
 
     def relay(h):
         copy13(h).wait_recv()
@@ -246,8 +242,9 @@
         cols = slice(a * rows, b * rows)
         s = s * (scale * math.log2(math.e)) + jnp.concatenate([bias[...]] * (b - a), axis=1)
         e = jnp.exp2(s - jnp.max(s, axis=0, keepdims=True))
-        p = e * (1.0 / jnp.sum(e, axis=0, keepdims=True))
-        delta = jnp.sum(p * dp, axis=0, keepdims=True)
+        inv = 1.0 / jnp.sum(e, axis=0, keepdims=True)
+        delta = jnp.sum(e * dp, axis=0, keepdims=True) * inv
+        p = e * inv
         ds_ref[:, cols] = (p * (dp - delta)).astype(BF16)
         p_ref[:, cols] = p.astype(BF16)
 
@@ -258,19 +255,22 @@
     def key_products(h, ds_ref, p_ref):
         dk = jnp.dot(ds_ref[...], qs[h], preferred_element_type=F32) * scale
         r0[h, 0] = dk[:rows]
-        rs13[h, 0, 0] = dk[rows : 2 * rows].astype(BF16)
-        r2[h, 0] = dk[2 * rows : 3 * rows]
+        r2[h, 0] = dk[rows : 2 * rows]
+        rs13[h, 0, 0] = dk[2 * rows : 3 * rows].astype(BF16)
         rs13[h, 1, 0] = dk[3 * rows :].astype(BF16)
+        return dk
+
+    def key_gains(h, dk):
         kpart = jnp.zeros((rows, HD), F32)
         for j in range(SEQ):
             kpart = kpart + unrot(dk[j * rows : (j + 1) * rows], j) * unrot(kv[h, j, 0].astype(F32), j)
-        gz[my_seq, pl.ds(nq + h, 1), :] = jnp.sum(kpart, axis=0, keepdims=True) / kgain[pl.ds(h, 1), :]
+        gz[my_seq, h, group : group + 1, :] = jnp.sum(kpart, axis=0, keepdims=True) / kgain[pl.ds(h, 1), :]
 
     def value_products(h, p_ref):
         dv = jnp.dot(p_ref[...], gs[h], preferred_element_type=F32)
         r0[h, 1] = dv[:rows]
-        rs13[h, 0, 1] = dv[rows : 2 * rows].astype(BF16)
-        r2[h, 1] = dv[2 * rows : 3 * rows]
+        r2[h, 1] = dv[rows : 2 * rows]
+        rs13[h, 0, 1] = dv[2 * rows : 3 * rows].astype(BF16)
         rs13[h, 1, 1] = dv[3 * rows :].astype(BF16)
 
     def query_products(h, ds_ref):
@@ -286,8 +286,18 @@
             w = dqn * qgain[pl.ds(h * group + g, 1), :]
             u[:, pl.ds(at, HD)] = w
             acc = acc + w * x
-            gz[my_seq, pl.ds(h * group + g, 1), :] = jnp.sum(dqn * x * rqb[...], axis=0, keepdims=True)
+            gz[my_seq, h, g : g + 1, :] = jnp.sum(dqn * x * rqb[...], axis=0, keepdims=True)
         accq[...] = acc
+
+    parts = (pl.ds(0, KVH - 1), pl.ds(KVH - 1, 1))
+
+    def z_copy(i, t):
+        mine = gz.at[my_seq, parts[t]]
+        return rcopy(mine, mine, s_z.at[t], r_z.at[t], zpeer[i])
+
+    def z_all(t):
+        others = gz.at[pl.ds(0, n_seq - 1), parts[t]]
+        return rcopy(others, others, s_z.at[t], r_z.at[t], zpeer[0])
 
     slots = ((ds_a, p_a), (ds_b, p_b))
 
@@ -296,12 +306,11 @@
         dq_t = query_products(h, now[0])
         weights(*sc, *chunks[0], *nxt)
         sc = scores(h + 1, *chunks[1])
-        key_products(h, *now)
+        dk = key_products(h, *now)
         query_side(h, dq_t)
         weights(*sc, *chunks[1], *nxt)
-        sc = scores(h + 1, *chunks[2])
         value_products(h, now[1])
-        weights(*sc, *chunks[2], *nxt)
+        key_gains(h, dk)
         copy13(h).start()
 
     def meet(h):
@@ -319,16 +328,17 @@
 
         @pl.when(i > 0)
         def _():
-            relay(h - 1)
+            relay(h - 2)
 
         step(h, slots[0], slots[1])
         meet(h + 2)
-        relay(h)
+
+        @pl.when(i > 0)
+        def _():
+            relay(h - 1)
+
         step(h + 1, slots[1], slots[0])
         return carry
-
-    half = (KVH - 2) // 2
-    lax.fori_loop(0, half, two, 0)
 
     @pl.when(lead)
     def _():
@@ -336,40 +346,50 @@
         for z in zpeer:
             tell(z_ready, z)
 
-    arrive(KVH - 1)
-    relay(KVH - 3)
-    step(KVH - 2, slots[0], slots[1])
+    half = (KVH - 2) // 2
+    lax.fori_loop(0, half, two, 0)
 
     @pl.when(lead)
     def _():
         pl.semaphore_wait(z_ready, n_seq - 1)
         tell(z_known, peer[1])
 
-    key_products(KVH - 1, *slots[1])
+    arrive(KVH - 1)
+    relay(KVH - 4)
+    step(KVH - 2, slots[0], slots[1])
+
+    @pl.when(jnp.logical_not(lead))
+    def _():
+        pl.semaphore_wait(z_known, 1)
+
+    for i in range(n_seq - 1):
+        z_copy(i, 0).start()
+    relay(KVH - 3)
+    dk_last = key_products(KVH - 1, *slots[1])
     value_products(KVH - 1, slots[1][1])
+    key_gains(KVH - 1, dk_last)
     copy13(KVH - 1).start()
     relay(KVH - 2)
     query_side(KVH - 1, query_products(KVH - 1, slots[1][0]))
 
-    @pl.when(jnp.logical_not(lead))
-    def _():
-        pl.semaphore_wait(z_known, 1)
-
     def gc_copy():
         return rcopy(gseq.at[0], gseq.at[1], s_g.at[0], r_g.at[0], peer[1])
 
     def gx_copy():
         return rcopy(gseq.at[2], gseq.at[3], s_g.at[1], r_g.at[1], peer[2])
 
-    def z_copy(i):
-        return rcopy(gz.at[my_seq], gz.at[my_seq], s_z.at[i], r_z.at[i], zpeer[i])
-
-    def z_recv(i):
-        src = lax.rem(my_seq + n_seq - 1 - i, n_seq)
-        return rcopy(gz.at[my_seq], gz.at[src], s_z.at[i], r_z.at[i], src * SEQ + rank)
+    def gl_copy(j):
+        return rcopy(glast.at[0], glast.at[j], s_l, r_l, peer[j])
+
+    def over_z(t):
+        z_all(t).wait_recv()
+        total = gz[0, parts[t]]
+        for s_i in range(1, n_seq):
+            total = total + gz[s_i, parts[t]]
+        return total
 
     for i in range(n_seq - 1):
-        z_copy(i).start()
+        z_copy(i, 1).start()
     relay(KVH - 1)
     rq = rqb[...]
     inner = jnp.sum(accq[...], axis=1, keepdims=True) / qw * rq * rq * rq
@@ -392,18 +412,20 @@
     early = KVH - 2
     for h in range(early):
         kacc = finish(h, kacc)
-
-    for i in range(n_seq - 1):
-        z_recv(i).wait_recv()
-    total = gz[0]
-    for s_i in range(1, n_seq):
-        total = total + gz[s_i]
-    gseq[0] = total
+    rcopy(kv.at[:, 0], kv.at[:, 1], s_x, r_x.at[0], peer[2]).wait_send()
+    rcopy(kv.at[:, 0], kv.at[:, 2], s_c, r_cf.at[0], peer[1]).wait_send()
+    rcopy(kv.at[:, 1], kv.at[:, 3], s_f, r_cf.at[0], peer[1]).wait_send()
+    rcopy(rs13, rr13, s_13, r_13.at[0], peer[1]).wait_send()
+
+    gseq[0] = over_z(0)
     gc_copy().start()
-    kacc = finish(early, kacc)
     gc_copy().wait_recv()
     gseq[2] = gseq[0] + gseq[1]
     gx_copy().start()
+    kacc = finish(early, kacc)
+    glast[0] = over_z(1)
+    for j in (2, 3, 1):
+        gl_copy(j).start()
     kacc = finish(early + 1, kacc)
 
     kinner = jnp.sum(kacc, axis=1, keepdims=True) / kw * rk * rk * rk
@@ -412,21 +434,22 @@
         kg_out[:, sl] = (rk * r2[h, 0] - k_in[:, sl].astype(F32) * kinner).astype(BF16)
 
     gx_copy().wait_recv()
-    total = gseq[2] + gseq[3]
-    qgg_out[...] = total[:nq]
-    kgg_out[...] = total[nq:]
-
+    gl_all = rcopy(glast.at[pl.ds(1, 3)], glast.at[pl.ds(1, 3)], s_l, r_l, peer[1])
+    gl_all.wait_recv()
     for h in range(KVH):
-        x_copy(h, 0).wait_send()
-        x_copy(h, 1).wait_send()
-        c_copy(h).wait_send()
-        f_copy(h).wait_send()
-        copy13(h).wait_send()
-        copy2(h).wait_send()
+        if h == KVH - 1:
+            rows_h = glast[0, 0] + glast[1, 0] + (glast[2, 0] + glast[3, 0])
+        else:
+            rows_h = gseq[2, h] + gseq[3, h]
+        qgg_out[h * group : (h + 1) * group, :] = rows_h[:group]
+        kgg_out[h : h + 1, :] = rows_h[group : group + 1]
+
+    rcopy(rs2, rr2, s_2, r_2.at[0], peer[2]).wait_send()
     gc_copy().wait_send()
     gx_copy().wait_send()
-    for i in range(n_seq - 1):
-        z_copy(i).wait_send()
+    gl_all.wait_send()
+    z_all(0).wait_send()
+    z_all(1).wait_send()
 
 
 def flush(*refs):
@@ -471,15 +494,15 @@
             pltpu.VMEM((nk, 2, 2, rows, HD), BF16),
             pltpu.VMEM((nk, 2, rows, HD), BF16),
             pltpu.VMEM((nk, 2, rows, HD), BF16),
-            pltpu.VMEM((SEQ, nq + nk, HD), F32),
-            pltpu.VMEM((n_seq, nq + nk, HD), F32),
+            pltpu.VMEM((SEQ, nk - 1, group + 1, HD), F32),
+            pltpu.VMEM((n_seq, nk, group + 1, HD), F32),
         ]
         + [pltpu.VMEM((SEQ * rows, group * rows), BF16)] * 4
         + [pltpu.VMEM((rows, HD), F32)] * 2
-        + [sem((nk, 2))] * 2
-        + [sem((nk,))] * 8
-        + [sem((2,))] * 2
-        + [sem((max(n_seq - 1, 1),))] * 2
+        + [pltpu.VMEM((SEQ, 1, group + 1, HD), F32)]
+        + [sem] * 7
+        + [sem((nk,))] * 4
+        + [sem((2,))] * 4
         + [
             pltpu.SMEM(layout.shape, jnp.int32),
             pltpu.VMEM((segments.shape[0] // HD, HD), jnp.int32),
@@ -491,7 +514,7 @@
             pltpu.VMEM(t_off.shape, F32),
             pltpu.VMEM(t_start.shape, F32),
             sem((9,)),
-            sem((nk,)),
+            sem,
         ]
         + [pltpu.SemaphoreType.REGULAR] * 3,
         compiler_params=pltpu.CompilerParams(

time: 41 us -> 32.1 us (0.78)
  Pallas kernels: 40.2 us -> 31.3 us
    pallas_call x1, Pallas kernels: 38.9 us -> 30 us  [body(): pl.pallas_call(functools.partial(kernel, n_seq), out_shape=(pltpu.VMEM((r...]
where the time goes in v2:
time: 32.1 us; the launch traced here: 31.9 us
  Pallas kernels  31.3 us (98%)
  between operations  0.64 us (2%)
    pallas_call x1, Pallas kernels, body(): pl.pallas_call(functools.partial(kernel, n_seq), out_shape=(pltpu.VMEM((r...  30 us
    pallas_call x1, Pallas kernels, body(): pl.pallas_call(flush, out_shape=tuple((jax.ShapeDtypeStruct(o.shape, o.dt...  1.27 us

profile of v2, /device:TPU:0, one launch (start us, length us, event | category | flops | bytes accessed | tf_op | source)
XLA Modules:
  0.0 31.9 jit_solution(9703983312790973479)
XLA Ops:
  0.6 30.0 %shard_map.137 = (bf16[128,5120]{1,0:T(8,128)(2,1)S(1)}, bf16[128,1024]{1,0:T(8,128)(2,1)S(1)}, bf16[128,1024]{1,0:T(8,128)(2,1)S(1)}, f32[40,128]{1,0:T(8,128)S(1)}, f32[8,128]{1,0:T(8,128)S(1)}) custom-call(s32[32]{0:T(128)} %layout_h.1, s32[16,128]{1,0:T(8,128)} %bitcast.6, bf16[128,5120]{1,0:T(8,128)(2,1)} %q_h.1, bf16[128,1024]{1,0:T(8,128)(2,1)} %k_h.1, ...), custom_call_target="tpu_custom_call" | custom-call | tf_op jit(solution)/shard_map/pallas_call | solution.py:473
  30.6 1.3 %shard_map.138 = (bf16[128,5120]{1,0:T(8,128)(2,1)}, bf16[128,1024]{1,0:T(8,128)(2,1)}, bf16[128,1024]{1,0:T(8,128)(2,1)}, f32[40,128]{1,0:T(8,128)}, f32[8,128]{1,0:T(8,128)}) custom-call(bf16[128,5120]{1,0:T(8,128)(2,1)S(1)} %get-tuple-element.15.refs_0_, bf16[128,1024]{1,0:T(8,128)(2,1)S(1)} %get-tuple-element.16.refs_1_, ...), custom_call_target="tpu_custom_call" | custom-call | tf_op jit(solution)/shard_map/pallas_call | solution.py:528

commit v3 on v2

--- a/solution.py
+++ b/solution.py
@@ -38,7 +38,7 @@
     n_seq,
     layout_h, seg_h, q_h, k_h, v_h, g_h, qgain_h, kgain_h, t_off_h, t_start_h,
     qg_out, kg_out, vg_out, qgg_out, kgg_out,
-    kv, bias, cs, qs, gs, u, r0, r2, rs13, rr13, rs2, rr2, gseq, gz, ds_a, p_a, ds_b, p_b, accq, rqb, glast,
+    kv, bias, cs, qs, gs, u, r0, r2, rs13, rr13, rs2, rr2, gseq, gz, ds_a, p_a, ds_b, p_b, accq, rqb, glast, glz,
     s_x, s_c, s_f, s_13, s_2, s_l, r_l, r_x, r_cf, r_13, r_2, s_g, r_g, s_z, r_z,
     layout, seg, q_in, k_in, g_in, qgain, kgain, t_off, t_start, l_sem, v_sem, ready, z_ready, z_known,
 ):
@@ -55,7 +55,8 @@
     rank = lax.rem(me, SEQ)
     base = me - rank
     my_seq = base // SEQ
-    lead = lax.rem(rank, 2) == 1
+    lead = lax.rem(rank, 2) == 0
+    near = lax.rem(rank, 2) == 1
 
     def flip(bit):
         if bit == 1:
@@ -289,15 +290,26 @@
             gz[my_seq, h, g : g + 1, :] = jnp.sum(dqn * x * rqb[...], axis=0, keepdims=True)
         accq[...] = acc
 
-    parts = (pl.ds(0, KVH - 1), pl.ds(KVH - 1, 1))
-
-    def z_copy(i, t):
-        mine = gz.at[my_seq, parts[t]]
-        return rcopy(mine, mine, s_z.at[t], r_z.at[t], zpeer[i])
-
-    def z_all(t):
-        others = gz.at[pl.ds(0, n_seq - 1), parts[t]]
-        return rcopy(others, others, s_z.at[t], r_z.at[t], zpeer[0])
+    early_rows = pl.ds(0, KVH - 2)
+    slot = my_seq * 2 + lax.rem(rank, 2)
+    side = [peer[1]]
+    for i in range(1, n_seq):
+        side += [zpeer[i - 1], zpeer[i - 1] - rank + flip(1)]
+
+    def z_copy(i):
+        mine = gz.at[my_seq, early_rows]
+        return rcopy(mine, mine, s_z.at[0], r_z.at[0], zpeer[i])
+
+    def z_all():
+        others = gz.at[pl.ds(0, n_seq - 1), early_rows]
+        return rcopy(others, others, s_z.at[0], r_z.at[0], zpeer[0])
+
+    def last_copy(dev):
+        return rcopy(gz.at[my_seq, pl.ds(KVH - 2, 2)], glz.at[slot], s_z.at[1], r_z.at[1], dev)
+
+    def last_all():
+        others = glz.at[pl.ds(0, 2 * n_seq - 1)]
+        return rcopy(others, others, s_z.at[1], r_z.at[1], peer[1])
 
     slots = ((ds_a, p_a), (ds_b, p_b))
 
@@ -324,6 +336,12 @@
 
     def two(i, carry):
         h = 2 * i
+
+        @pl.when(jnp.logical_and(lead, i == half - 1))
+        def _():
+            pl.semaphore_wait(z_ready, n_seq - 1)
+            tell(z_known, peer[1])
+
         meet(h + 1)
 
         @pl.when(i > 0)
@@ -349,28 +367,26 @@
     half = (KVH - 2) // 2
     lax.fori_loop(0, half, two, 0)
 
-    @pl.when(lead)
-    def _():
-        pl.semaphore_wait(z_ready, n_seq - 1)
-        tell(z_known, peer[1])
-
+    @pl.when(jnp.logical_not(lead))
+    def _():
+        pl.semaphore_wait(z_known, 1)
+
+    for i in range(n_seq - 1):
+        z_copy(i).start()
     arrive(KVH - 1)
     relay(KVH - 4)
     step(KVH - 2, slots[0], slots[1])
 
-    @pl.when(jnp.logical_not(lead))
-    def _():
-        pl.semaphore_wait(z_known, 1)
-
-    for i in range(n_seq - 1):
-        z_copy(i, 0).start()
     relay(KVH - 3)
     dk_last = key_products(KVH - 1, *slots[1])
+    query_side(KVH - 1, query_products(KVH - 1, slots[1][0]))
+    key_gains(KVH - 1, dk_last)
+    glz[slot] = gz[my_seq, KVH - 2 :]
+    for dev in side:
+        last_copy(dev).start()
+    relay(KVH - 2)
     value_products(KVH - 1, slots[1][1])
-    key_gains(KVH - 1, dk_last)
     copy13(KVH - 1).start()
-    relay(KVH - 2)
-    query_side(KVH - 1, query_products(KVH - 1, slots[1][0]))
 
     def gc_copy():
         return rcopy(gseq.at[0], gseq.at[1], s_g.at[0], r_g.at[0], peer[1])
@@ -379,17 +395,8 @@
         return rcopy(gseq.at[2], gseq.at[3], s_g.at[1], r_g.at[1], peer[2])
 
     def gl_copy(j):
-        return rcopy(glast.at[0], glast.at[j], s_l, r_l, peer[j])
-
-    def over_z(t):
-        z_all(t).wait_recv()
-        total = gz[0, parts[t]]
-        for s_i in range(1, n_seq):
-            total = total + gz[s_i, parts[t]]
-        return total
-
-    for i in range(n_seq - 1):
-        z_copy(i, 1).start()
+        return rcopy(glast.at[0], glast.at[1], s_l, r_l, peer[j])
+
     relay(KVH - 1)
     rq = rqb[...]
     inner = jnp.sum(accq[...], axis=1, keepdims=True) / qw * rq * rq * rq
@@ -409,47 +416,64 @@
         r2[h, 0] = w
         return kacc + w * x
 
-    early = KVH - 2
-    for h in range(early):
-        kacc = finish(h, kacc)
     rcopy(kv.at[:, 0], kv.at[:, 1], s_x, r_x.at[0], peer[2]).wait_send()
     rcopy(kv.at[:, 0], kv.at[:, 2], s_c, r_cf.at[0], peer[1]).wait_send()
     rcopy(kv.at[:, 1], kv.at[:, 3], s_f, r_cf.at[0], peer[1]).wait_send()
     rcopy(rs13, rr13, s_13, r_13.at[0], peer[1]).wait_send()
 
-    gseq[0] = over_z(0)
+    for h in range(3):
+        kacc = finish(h, kacc)
+    z_all().wait_recv()
+    total = gz[0, early_rows]
+    for s_i in range(1, n_seq):
+        total = total + gz[s_i, early_rows]
+    gseq[0] = total
     gc_copy().start()
+    kacc = finish(3, kacc)
+    kacc = finish(4, kacc)
     gc_copy().wait_recv()
     gseq[2] = gseq[0] + gseq[1]
     gx_copy().start()
-    kacc = finish(early, kacc)
-    glast[0] = over_z(1)
-    for j in (2, 3, 1):
-        gl_copy(j).start()
-    kacc = finish(early + 1, kacc)
+    kacc = finish(KVH - 3, kacc)
+    last_all().wait_recv()
+    last = glz[0]
+    for s_i in range(1, 2 * n_seq):
+        last = last + glz[s_i]
+    glast[0] = last
+
+    @pl.when(near)
+    def _():
+        gl_copy(2).start()
+        gl_copy(3).start()
+
+    kacc = finish(KVH - 2, kacc)
+    kacc = finish(KVH - 1, kacc)
 
     kinner = jnp.sum(kacc, axis=1, keepdims=True) / kw * rk * rk * rk
     for h in range(KVH):
         sl = slice(h * HD, (h + 1) * HD)
         kg_out[:, sl] = (rk * r2[h, 0] - k_in[:, sl].astype(F32) * kinner).astype(BF16)
 
-    gx_copy().wait_recv()
-    gl_all = rcopy(glast.at[pl.ds(1, 3)], glast.at[pl.ds(1, 3)], s_l, r_l, peer[1])
-    gl_all.wait_recv()
-    for h in range(KVH):
-        if h == KVH - 1:
-            rows_h = glast[0, 0] + glast[1, 0] + (glast[2, 0] + glast[3, 0])
-        else:
-            rows_h = gseq[2, h] + gseq[3, h]
+    rcopy(rs2, rr2, s_2, r_2.at[0], peer[2]).wait_send()
+    gc_copy().wait_send()
+    z_all().wait_send()
+    last_all().wait_send()
+
+    def gains(h, rows_h):
         qgg_out[h * group : (h + 1) * group, :] = rows_h[:group]
         kgg_out[h : h + 1, :] = rows_h[group : group + 1]
 
-    rcopy(rs2, rr2, s_2, r_2.at[0], peer[2]).wait_send()
-    gc_copy().wait_send()
+    gx_copy().wait_recv()
+    for h in range(KVH - 2):
+        gains(h, gseq[2, h] + gseq[3, h])
     gx_copy().wait_send()
-    gl_all.wait_send()
-    z_all(0).wait_send()
-    z_all(1).wait_send()
+    gl_copy(2).wait_recv()
+    for h in range(2):
+        gains(KVH - 2 + h, glast[0, h] + glast[1, h])
+
+    @pl.when(near)
+    def _():
+        rcopy(glast, glast, s_l, r_l, peer[2]).wait_send()
 
 
 def flush(*refs):
@@ -494,12 +518,12 @@
             pltpu.VMEM((nk, 2, 2, rows, HD), BF16),
             pltpu.VMEM((nk, 2, rows, HD), BF16),
             pltpu.VMEM((nk, 2, rows, HD), BF16),
-            pltpu.VMEM((SEQ, nk - 1, group + 1, HD), F32),
+            pltpu.VMEM((SEQ, nk - 2, group + 1, HD), F32),
             pltpu.VMEM((n_seq, nk, group + 1, HD), F32),
         ]
         + [pltpu.VMEM((SEQ * rows, group * rows), BF16)] * 4
         + [pltpu.VMEM((rows, HD), F32)] * 2
-        + [pltpu.VMEM((SEQ, 1, group + 1, HD), F32)]
+        + [pltpu.VMEM((2, 2, group + 1, HD), F32), pltpu.VMEM((2 * n_seq, 2, group + 1, HD), F32)]
         + [sem] * 7
         + [sem((nk,))] * 4
         + [sem((2,))] * 4

time: 32.1 us -> 31.1 us (0.969)
  Pallas kernels: 31.3 us -> 30.3 us
    pallas_call x1, Pallas kernels: 30 us -> 29 us  [body(): pl.pallas_call(functools.partial(kernel, n_seq), out_shape=(pltpu.VMEM((r...]
where the time goes in v3:
time: 31.1 us; the launch traced here: 31 us
  Pallas kernels  30.3 us (97%)
  between operations  0.64 us (2%)
    pallas_call x1, Pallas kernels, body(): pl.pallas_call(functools.partial(kernel, n_seq), out_shape=(pltpu.VMEM((r...  29 us
    pallas_call x1, Pallas kernels, body(): pl.pallas_call(flush, out_shape=tuple((jax.ShapeDtypeStruct(o.shape, o.dt...  1.27 us

profile of v3, /device:TPU:0, one launch (start us, length us, event | category | flops | bytes accessed | tf_op | source)
XLA Modules:
  0.0 31.0 jit_solution(6849841626555499501)
XLA Ops:
  0.6 29.0 %shard_map.137 = (bf16[128,5120]{1,0:T(8,128)(2,1)S(1)}, bf16[128,1024]{1,0:T(8,128)(2,1)S(1)}, bf16[128,1024]{1,0:T(8,128)(2,1)S(1)}, f32[40,128]{1,0:T(8,128)S(1)}, f32[8,128]{1,0:T(8,128)S(1)}) custom-call(s32[32]{0:T(128)} %layout_h.1, s32[16,128]{1,0:T(8,128)} %bitcast.6, bf16[128,5120]{1,0:T(8,128)(2,1)} %q_h.1, bf16[128,1024]{1,0:T(8,128)(2,1)} %k_h.1, ...), custom_call_target="tpu_custom_call" | custom-call | tf_op jit(solution)/shard_map/pallas_call | solution.py:497
  29.7 1.3 %shard_map.138 = (bf16[128,5120]{1,0:T(8,128)(2,1)}, bf16[128,1024]{1,0:T(8,128)(2,1)}, bf16[128,1024]{1,0:T(8,128)(2,1)}, f32[40,128]{1,0:T(8,128)}, f32[8,128]{1,0:T(8,128)}) custom-call(bf16[128,5120]{1,0:T(8,128)(2,1)S(1)} %get-tuple-element.15.refs_0_, bf16[128,1024]{1,0:T(8,128)(2,1)S(1)} %get-tuple-element.16.refs_1_, ...), custom_call_target="tpu_custom_call" | custom-call | tf_op jit(solution)/shard_map/pallas_call | solution.py:552

commit v4 on v3

--- a/solution.py
+++ b/solution.py
@@ -14,7 +14,7 @@
 SEQ = 4
 LENGTH = 512
 EPS = 1e-06
-AHEAD = 2
+AHEAD = 1
 CHUNK = 3
 BASE = 500000.0
 F32 = jnp.float32
@@ -377,13 +377,14 @@
     relay(KVH - 4)
     step(KVH - 2, slots[0], slots[1])
 
-    relay(KVH - 3)
+    dq_last = query_products(KVH - 1, slots[1][0])
     dk_last = key_products(KVH - 1, *slots[1])
-    query_side(KVH - 1, query_products(KVH - 1, slots[1][0]))
+    query_side(KVH - 1, dq_last)
     key_gains(KVH - 1, dk_last)
     glz[slot] = gz[my_seq, KVH - 2 :]
     for dev in side:
         last_copy(dev).start()
+    relay(KVH - 3)
     relay(KVH - 2)
     value_products(KVH - 1, slots[1][1])
     copy13(KVH - 1).start()

time: 31.1 us -> 31.1 us (level)
  no operation moved by 1% of the time
where the time goes in v4:
time: 31.1 us; the launch traced here: 30.9 us
  Pallas kernels  30.3 us (97%)
  between operations  0.64 us (2%)
    pallas_call x1, Pallas kernels, body(): pl.pallas_call(functools.partial(kernel, n_seq), out_shape=(pltpu.VMEM((r...  29 us
    pallas_call x1, Pallas kernels, body(): pl.pallas_call(flush, out_shape=tuple((jax.ShapeDtypeStruct(o.shape, o.dt...  1.27 us

profile of v4, /device:TPU:0, one launch (start us, length us, event | category | flops | bytes accessed | tf_op | source)
XLA Modules:
  0.0 30.9 jit_solution(14334674064278187698)
XLA Ops:
  0.6 29.0 %shard_map.137 = (bf16[128,5120]{1,0:T(8,128)(2,1)S(1)}, bf16[128,1024]{1,0:T(8,128)(2,1)S(1)}, bf16[128,1024]{1,0:T(8,128)(2,1)S(1)}, f32[40,128]{1,0:T(8,128)S(1)}, f32[8,128]{1,0:T(8,128)S(1)}) custom-call(s32[32]{0:T(128)} %layout_h.1, s32[16,128]{1,0:T(8,128)} %bitcast.6, bf16[128,5120]{1,0:T(8,128)(2,1)} %q_h.1, bf16[128,1024]{1,0:T(8,128)(2,1)} %k_h.1, ...), custom_call_target="tpu_custom_call" | custom-call | tf_op jit(solution)/shard_map/pallas_call | solution.py:498
  29.6 1.3 %shard_map.138 = (bf16[128,5120]{1,0:T(8,128)(2,1)}, bf16[128,1024]{1,0:T(8,128)(2,1)}, bf16[128,1024]{1,0:T(8,128)(2,1)}, f32[40,128]{1,0:T(8,128)}, f32[8,128]{1,0:T(8,128)}) custom-call(bf16[128,5120]{1,0:T(8,128)(2,1)S(1)} %get-tuple-element.15.refs_0_, bf16[128,1024]{1,0:T(8,128)(2,1)S(1)} %get-tuple-element.16.refs_1_, ...), custom_call_target="tpu_custom_call" | custom-call | tf_op jit(solution)/shard_map/pallas_call | solution.py:553
